TPU v7x, 32 devices: a whole 2x2x4 slice. The times are simulated.
32 devices in a mesh: dp: 8 (over z, x), expert: 4 (over y, core).
Axes of the slice: x: 2, y: 2, z: 4, core: 2. Of those that a mesh axis runs over, the one named last changes fastest.
Arguments:
- tokens: bfloat16 [4096, 1024], P(('dp', 'expert')), may hold values from -24 to 24
- cotangent: bfloat16 [4096, 1024], P(('dp', 'expert')), may hold values from -6 to 6
- prefix: int32 [8], P('dp'), may hold values from 51 to 256
- expert_choice: int32 [4096, 1], P(('dp', 'expert')), may hold values from 0 to 3; in each aligned block of 128 rows (0 to 127, 128 to 255, ...) at most 64 rows name the same one
- norm1_gain: bfloat16 [1024], P(('dp', 'expert')), may hold values from 0.099609375 to 1.8984375
- w_qkv: bfloat16 [1024, 3072], P(('dp', 'expert')), may hold values from -0.1875 to 0.1875
- w_out: bfloat16 [1024, 1024], P(('dp', 'expert')), may hold values from -1.5 to 1.5
- norm2_gain: bfloat16 [1024], P(('dp', 'expert')), may hold values from 0.099609375 to 1.8984375
- w_up: bfloat16 [1024, 4096], P(('dp', 'expert')), may hold values from -0.1875 to 0.1875
- w_down: bfloat16 [4096, 1024], P(('dp', 'expert')), may hold values from -0.09375 to 0.09375
- w_router: bfloat16 [1024, 4], P(('dp', 'expert')), may hold values from -0.125 to 0.125
- w_mix: bfloat16 [1024, 2], P(('dp', 'expert')), may hold values from -0.1875 to 0.1875
- expert_up: bfloat16 [4096, 4, 1024], P('dp', 'expert'), may hold values from -0.1875 to 0.1875
- expert_down: bfloat16 [4096, 4, 1024], P('dp', 'expert'), may hold values from -0.375 to 0.375
Outputs:
- output: float32 [4096, 1024], P(('dp', 'expert'))
- grad_tokens: float32 [4096, 1024], P(('dp', 'expert'))
- grad_norm1_gain: float32 [1024], P(('dp', 'expert'))
- grad_w_qkv: float32 [1024, 3072], P(('dp', 'expert'))
- grad_w_out: float32 [1024, 1024], P(('dp', 'expert'))
- grad_norm2_gain: float32 [1024], P(('dp', 'expert'))
- grad_w_up: float32 [1024, 4096], P(('dp', 'expert'))
- grad_w_down: float32 [4096, 1024], P(('dp', 'expert'))
- grad_w_router: float32 [1024, 4], P(('dp', 'expert'))
- grad_w_mix: float32 [1024, 2], P(('dp', 'expert'))
- grad_expert_up: float32 [4096, 4, 1024], P('dp', 'expert')
- grad_expert_down: float32 [4096, 4, 1024], P('dp', 'expert')
- rms_mid: float32 [], replicated
- rms_attn: float32 [], replicated
- rms_ffn: float32 [], replicated
- rms_out: float32 [], replicated
Inputs may be any that keep to these rules, and one draw needn't show every extreme that they name: `expert_choice`: among the 128 rows of one device no expert is chosen more than 64 times.
All inputs are finite; a program needn't handle non-finite values.
Results may differ from a plain program's by a relative error of at most 0.033.
Values may be sent and summed in bfloat16 or wider, within the bound.
A program may use at most 192 MiB of HBM per device.

v0:
```python
import jax
import jax.numpy as jnp
from jax import lax
from jax.sharding import PartitionSpec as P

HEAD = 64
EPS = 1e-05
NEG_FILL = -1e30
HIGHEST = lax.Precision.HIGHEST
ROWS_AXIS = (((0,), (0,)), ((), ()))
COLS_AXIS = (((1,), (1,)), ((), ()))


def layer_norm(values, norm_gain):
    row_mean = jnp.mean(values, axis=-1, keepdims=True)
    centered = values - row_mean
    inverse = lax.rsqrt(jnp.mean(centered * centered, axis=-1, keepdims=True) + EPS)
    normed = centered * inverse
    return (normed * norm_gain, normed, inverse)


def norm_back(grad_out, normed, inverse, norm_gain):
    scaled = grad_out * norm_gain
    mean_one = jnp.mean(scaled, axis=-1, keepdims=True)
    mean_two = jnp.mean(scaled * normed, axis=-1, keepdims=True)
    return (inverse * (scaled - mean_one - normed * mean_two), jnp.sum(grad_out * normed, axis=0))


def gelu_tanh(values):
    return jax.nn.gelu(values, approximate=True)


def gelu_back(pre_act, grad_act):
    return jax.vjp(gelu_tanh, pre_act)[1](grad_act)[0]


def softmax_rows(logits):
    shifted = logits - jnp.max(logits, axis=-1, keepdims=True)
    weights = jnp.exp(shifted)
    return weights / jnp.sum(weights, axis=-1, keepdims=True)


def contract_rows(left_side, right_side):
    return lax.dot_general(left_side, right_side, ROWS_AXIS, preferred_element_type=jnp.float32)


def contract_cols(left_side, right_side):
    return lax.dot_general(left_side, right_side, COLS_AXIS, preferred_element_type=jnp.float32)


def precise_rows(left_side, right_side):
    return lax.dot_general(
        left_side, right_side, ROWS_AXIS, precision=HIGHEST, preferred_element_type=jnp.float32
    )


def precise_cols(left_side, right_side):
    return lax.dot_general(
        left_side, right_side, COLS_AXIS, precision=HIGHEST, preferred_element_type=jnp.float32
    )


def per_device(
    tokens,
    cotangent,
    prefix,
    expert_choice,
    norm1_gain,
    w_qkv,
    w_out,
    norm2_gain,
    w_up,
    w_down,
    w_router,
    w_mix,
    expert_up,
    expert_down,
):
    local_rows, model_width = tokens.shape
    experts = lax.axis_size("expert")
    replicas = lax.axis_size("dp")
    capacity = 2 * local_rows // experts
    cut_width = model_width // experts
    head_count = cut_width // HEAD
    ff_cut = w_up.shape[1] // experts
    row_share = w_qkv.shape[0]
    ff_share = w_down.shape[0]
    stride = replicas // experts
    my_block = lax.axis_index("dp") * experts + lax.axis_index("expert")
    score_scale = HEAD ** (-0.5)
    ff_own = replicas * ff_share

    def spread(rows_low):
        return lax.all_gather(rows_low, "expert", axis=0, tiled=True)

    def fold(partial_sums):
        return lax.psum_scatter(
            partial_sums.astype(jnp.bfloat16), "expert", scatter_dimension=0, tiled=True
        ).astype(jnp.float32)

    def swap(blocks):
        return lax.all_to_all(blocks, "expert", split_axis=0, concat_axis=0, tiled=True)

    def gather_dp(rows):
        return lax.all_gather(rows, "dp", axis=0, tiled=True)

    def scatter_dp(rows):
        return lax.psum_scatter(rows.astype(jnp.bfloat16), "dp", scatter_dimension=0, tiled=True)

    small = lax.all_gather(
        jnp.concatenate([norm1_gain[:, None], norm2_gain[:, None], w_router, w_mix], axis=1),
        ("dp", "expert"),
        axis=0,
        tiled=True,
    )
    gain_one = small[:, 0].astype(jnp.float32)
    gain_two = small[:, 1].astype(jnp.float32)
    router_w = small[:, 2 : 2 + experts]
    mix_w = small[:, 2 + experts :]
    qkv_out = jnp.moveaxis(w_qkv.reshape(row_share, 3, experts, cut_width), 2, 0)
    qkv_w = gather_dp(swap(qkv_out).reshape(experts * row_share, 3 * cut_width))
    out_rows = gather_dp(w_out)
    out_in = swap(out_rows.reshape(experts, stride * row_share, model_width))
    out_w = jnp.transpose(
        out_in.reshape(experts, stride, row_share, model_width), (1, 0, 2, 3)
    ).reshape(cut_width, model_width)
    up_out = jnp.moveaxis(w_up.reshape(row_share, replicas, experts, ff_share), 2, 0)
    up_w = gather_dp(swap(up_out).reshape(experts * row_share, ff_own))
    down_w = gather_dp(w_down)
    expert_in_w = expert_up[:, 0, :]
    expert_out_w = expert_down[:, 0, :]
    inputs = tokens.astype(jnp.float32)
    scaled_one, normed_one, inverse_one = layer_norm(inputs, gain_one)
    normed_all = spread(scaled_one.astype(jnp.bfloat16))
    seq_len = normed_all.shape[0]
    qkv_cut = jnp.dot(normed_all, qkv_w, preferred_element_type=jnp.float32).astype(jnp.bfloat16)
    queries = qkv_cut[:, :cut_width].reshape(seq_len, head_count, HEAD)
    keys = qkv_cut[:, cut_width : 2 * cut_width].reshape(seq_len, head_count, HEAD)
    values = qkv_cut[:, 2 * cut_width :].reshape(seq_len, head_count, HEAD)
    position = jnp.arange(seq_len, dtype=jnp.int32)
    visible = (position[None, :] <= position[:, None]) | (position[None, :] < prefix[0])
    masked = jnp.where(
        visible[None],
        jnp.einsum("qhd,khd->hqk", queries, keys, preferred_element_type=jnp.float32) * score_scale,
        NEG_FILL,
    )
    row_max = jnp.max(masked, axis=-1, keepdims=True)
    expd = jnp.exp(masked - row_max)
    probs = expd / jnp.sum(expd, axis=-1, keepdims=True)
    probs_low = probs.astype(jnp.bfloat16)
    attended_cut = (
        jnp.einsum("hqk,khd->qhd", probs_low, values, preferred_element_type=jnp.float32)
        .reshape(seq_len, cut_width)
        .astype(jnp.bfloat16)
    )
    attn_out = fold(jnp.dot(attended_cut, out_w, preferred_element_type=jnp.float32))
    middle = inputs + attn_out
    scaled_two, normed_two, inverse_two = layer_norm(middle, gain_two)
    hidden_low = scaled_two.astype(jnp.bfloat16)
    router_probs = softmax_rows(jnp.dot(hidden_low, router_w, preferred_element_type=jnp.float32))
    chosen = expert_choice[:, 0]
    onehot_int = (jnp.arange(experts, dtype=jnp.int32)[None, :] == chosen[:, None]).astype(
        jnp.int32
    )
    onehot = onehot_int.astype(jnp.float32)
    gate_prob = jnp.sum(router_probs * onehot, axis=-1)
    mix_coef = softmax_rows(jnp.dot(hidden_low, mix_w, preferred_element_type=jnp.float32))
    coef_dense = mix_coef[:, 0:1]
    coef_expert = (mix_coef[:, 1] * gate_prob)[:, None]
    grad_out = cotangent.astype(jnp.float32)
    grad_dense = (grad_out * coef_dense).astype(jnp.bfloat16)
    grad_expert = (grad_out * coef_expert).astype(jnp.bfloat16)
    row_id = jnp.arange(local_rows, dtype=jnp.int32)
    before = (row_id[:, None] > row_id[None, :]).astype(jnp.bfloat16)
    earlier = jnp.dot(before, onehot.astype(jnp.bfloat16), preferred_element_type=jnp.float32)
    slot_rank = jnp.sum(earlier * onehot, axis=-1).astype(jnp.int32)
    slot_index = chosen * capacity + slot_rank
    slot_rows = experts * capacity
    picks = (slot_index[:, None] == jnp.arange(slot_rows, dtype=jnp.int32)[None, :]).astype(
        jnp.bfloat16
    )
    send_rows = contract_rows(picks, jnp.concatenate([hidden_low, grad_expert], axis=1)).astype(
        jnp.bfloat16
    )
    received = swap(send_rows.reshape(experts, capacity, 2 * model_width))
    routed = gather_dp(received.reshape(slot_rows, 2 * model_width))
    routed_in = routed[:, :model_width]
    routed_grad = routed[:, model_width:]
    dense_rows = spread(jnp.concatenate([hidden_low, grad_dense], axis=1))
    hidden_all = dense_rows[:, :model_width]
    grad_dense_all = dense_rows[:, model_width:]
    dense_pre = jnp.dot(hidden_all, up_w, preferred_element_type=jnp.float32)
    dense_act = gelu_tanh(dense_pre).astype(jnp.bfloat16)
    grad_act_d = contract_cols(grad_dense_all, down_w)
    grad_pre_d = gelu_back(dense_pre, grad_act_d).astype(jnp.bfloat16)
    dense_sums = jnp.concatenate(
        [
            jnp.dot(dense_act, down_w, preferred_element_type=jnp.float32).astype(jnp.bfloat16),
            contract_cols(grad_pre_d, up_w).astype(jnp.bfloat16),
        ],
        axis=1,
    )
    dense_back = fold(dense_sums)
    dense_out = dense_back[:, :model_width]
    grad_w_down_cut = contract_rows(dense_act, grad_dense_all)
    grad_w_up_cut = contract_rows(hidden_all, grad_pre_d)
    pre_act = contract_cols(routed_in, expert_in_w)
    act_low = gelu_tanh(pre_act).astype(jnp.bfloat16)
    grad_act_e = contract_cols(routed_grad, expert_out_w)
    grad_pre_e = gelu_back(pre_act, grad_act_e).astype(jnp.bfloat16)
    expert_sums = jnp.concatenate(
        [
            jnp.dot(act_low, expert_out_w, preferred_element_type=jnp.float32).astype(jnp.bfloat16),
            jnp.dot(grad_pre_e, expert_in_w, preferred_element_type=jnp.float32).astype(
                jnp.bfloat16
            ),
        ],
        axis=1,
    )
    grad_expert_up = contract_rows(grad_pre_e, routed_in)
    grad_expert_down = contract_rows(act_low, routed_grad)
    expert_back = swap(scatter_dp(expert_sums).reshape(experts, capacity, 2 * model_width))
    expert_rows_all = jnp.dot(
        picks, expert_back.reshape(slot_rows, 2 * model_width), preferred_element_type=jnp.float32
    )
    expert_rows = expert_rows_all[:, :model_width]
    ffn_out = coef_dense * dense_out + coef_expert * expert_rows
    result = middle + ffn_out
    square_stats = jnp.stack(
        [
            jnp.sum(middle * middle),
            jnp.sum(attn_out * attn_out),
            jnp.sum(ffn_out * ffn_out),
            jnp.sum(result * result),
        ]
    )
    dense_dot = jnp.sum(grad_out * dense_out, axis=-1)
    expert_dot = jnp.sum(grad_out * expert_rows, axis=-1)
    coef_grad = jnp.stack([dense_dot, expert_dot * gate_prob], axis=-1)
    grad_mix = mix_coef * (coef_grad - jnp.sum(mix_coef * coef_grad, axis=-1, keepdims=True))
    gate_grad = expert_dot * mix_coef[:, 1]
    grad_router = (gate_grad * gate_prob)[:, None] * (onehot - router_probs)
    hidden_wide = hidden_low.astype(jnp.float32)
    grad_hidden = dense_back[:, model_width:] + expert_rows_all[:, model_width:]
    grad_hidden = (
        grad_hidden
        + precise_cols(grad_router, router_w.astype(jnp.float32))
        + precise_cols(grad_mix, mix_w.astype(jnp.float32))
    )
    grad_w_router = precise_rows(grad_router, hidden_wide)
    grad_w_mix = precise_rows(grad_mix, hidden_wide)
    grad_mid_norm, grad_gain_two = norm_back(grad_hidden, normed_two, inverse_two, gain_two)
    grad_middle = grad_out + grad_mid_norm
    grad_attn_all = spread(grad_middle.astype(jnp.bfloat16))
    grad_w_out_cut = contract_rows(attended_cut, grad_attn_all)
    grad_att_cut = (
        contract_cols(grad_attn_all, out_w).astype(jnp.bfloat16).reshape(seq_len, head_count, HEAD)
    )
    grad_probs = jnp.einsum(
        "qhd,khd->hqk", grad_att_cut, values, preferred_element_type=jnp.float32
    )
    row_delta = jnp.sum(probs * grad_probs, axis=-1, keepdims=True)
    grad_scores = (probs * (grad_probs - row_delta)).astype(jnp.bfloat16)
    grad_query = (
        jnp.einsum("hqk,khd->qhd", grad_scores, keys, preferred_element_type=jnp.float32)
        * score_scale
    )
    grad_key = (
        jnp.einsum("hqk,qhd->khd", grad_scores, queries, preferred_element_type=jnp.float32)
        * score_scale
    )
    grad_value = jnp.einsum(
        "hqk,qhd->khd", probs_low, grad_att_cut, preferred_element_type=jnp.float32
    )
    grad_qkv_cut = jnp.concatenate(
        [
            grad_query.reshape(seq_len, cut_width),
            grad_key.reshape(seq_len, cut_width),
            grad_value.reshape(seq_len, cut_width),
        ],
        axis=1,
    ).astype(jnp.bfloat16)
    grad_w_qkv_cut = contract_rows(normed_all, grad_qkv_cut)
    grad_normed = fold(contract_cols(grad_qkv_cut, qkv_w))
    grad_in_norm, grad_gain_one = norm_back(grad_normed, normed_one, inverse_one, gain_one)
    grad_tokens = grad_middle + grad_in_norm
    up_sum = swap(scatter_dp(grad_w_up_cut).reshape(experts, row_share, replicas, ff_share))
    grad_w_up = (
        jnp.transpose(up_sum, (1, 2, 0, 3)).reshape(row_share, experts * ff_own).astype(jnp.float32)
    )
    grad_w_down = scatter_dp(grad_w_down_cut).astype(jnp.float32)
    out_send = jnp.transpose(
        grad_w_out_cut.astype(jnp.bfloat16).reshape(stride, experts, row_share, model_width),
        (1, 0, 2, 3),
    )
    grad_w_out = scatter_dp(swap(out_send).reshape(replicas * row_share, model_width)).astype(
        jnp.float32
    )
    qkv_sum = swap(scatter_dp(grad_w_qkv_cut).reshape(experts, row_share, 3, cut_width))
    grad_w_qkv = (
        jnp.transpose(qkv_sum, (1, 2, 0, 3)).reshape(row_share, 3 * model_width).astype(jnp.float32)
    )
    totals = lax.psum(
        (
            jnp.concatenate(
                [grad_gain_one[None], grad_gain_two[None], grad_w_router, grad_w_mix], axis=0
            ),
            square_stats,
        ),
        ("dp", "expert"),
    )
    own = lax.dynamic_slice_in_dim(totals[0], my_block * row_share, row_share, 1)
    entry_count = local_rows * model_width * replicas * experts
    rms_values = jnp.sqrt(totals[1] / entry_count + 1e-06)
    return (
        result,
        grad_tokens,
        own[0],
        grad_w_qkv,
        grad_w_out,
        own[1],
        grad_w_up,
        grad_w_down,
        jnp.transpose(own[2 : 2 + experts]),
        jnp.transpose(own[2 + experts :]),
        grad_expert_up[:, None, :],
        grad_expert_down[:, None, :],
        rms_values[0],
        rms_values[1],
        rms_values[2],
        rms_values[3],
    )


def solution(mesh):
    return jax.shard_map(
        per_device,
        mesh=mesh,
        in_specs=(
            P(("dp", "expert"), None),
            P(("dp", "expert"), None),
            P("dp"),
            P(("dp", "expert"), None),
            P(("dp", "expert")),
            P(("dp", "expert"), None),
            P(("dp", "expert"), None),
            P(("dp", "expert")),
            P(("dp", "expert"), None),
            P(("dp", "expert"), None),
            P(("dp", "expert"), None),
            P(("dp", "expert"), None),
            P("dp", "expert", None),
            P("dp", "expert", None),
        ),
        out_specs=(
            P(("dp", "expert"), None),
            P(("dp", "expert"), None),
            P(("dp", "expert")),
            P(("dp", "expert"), None),
            P(("dp", "expert"), None),
            P(("dp", "expert")),
            P(("dp", "expert"), None),
            P(("dp", "expert"), None),
            P(("dp", "expert"), None),
            P(("dp", "expert"), None),
            P("dp", "expert", None),
            P("dp", "expert", None),
            P(),
            P(),
            P(),
            P(),
        ),
        check_vma=False,
    )
```

profile of v0, /device:TPU:0, one launch (start us, length us, event | category | flops | bytes accessed | tf_op | source)
XLA Modules:
  0.0 951.4 jit_solution(9734725191694061075)
XLA Ops:
  10.3 43.4 %all-gather = bf16[32,32,8]{1,2,0:T(8,128)(2,1)S(1)} all-gather(bf16[1,32,8]{1,2,0:T(8,128)(2,1)S(1)} %maximum_bitcast_fusion), channel_id=1, replica_groups=mesh['dp'=8,'expert'=4] {'dp','expert'}, dimensions={0}, use_global_device_ids=true | all-gather | bytes 16896 | tf_op jit(solution)/shard_map/all_gather | solution.py:110
  56.9 10.1 %all_to_all.40 = bf16[4,32,3,256]{3,1,2,0:T(8,128)(2,1)S(1)} all-to-all(bf16[4,32,3,256]{3,1,2,0:T(8,128)(2,1)S(1)} %copy.96), channel_id=1, replica_groups=mesh['dp'=8,'expert'=4] {'expert'}, dimensions={0} | all-to-all | bytes 393216 | tf_op jit(solution)/shard_map/all_to_all | solution.py:102
  67.9 33.8 %all_gather.30 = bf16[256,1024]{1,0:T(8,128)(2,1)} all-gather(bf16[32,1024]{1,0:T(8,128)(2,1)S(1)} %copy-done.26), channel_id=1, replica_groups=mesh['dp'=8,'expert'=4] {'dp'}, dimensions={0}, use_global_device_ids=true | all-gather | bytes 589824 | tf_op jit(solution)/shard_map/all_gather | solution.py:105
  101.7 3.5 all-to-all-start.1
  106.0 7.9 all-to-all-done.1
  114.1 2.3 all-gather.11.cloned.1.call-done
  116.4 2.7 convolution_convert_fusion.10
  119.6 3.6 fusion.112
  123.3 2.7 convolution_convert_fusion.14
  128.3 23.1 %reduce-scatter.9.cloned.1.call-done = bf16[128,1024]{1,0:T(8,128)(2,1)} async-done(((bf16[512,1024]{1,0:T(8,128)(2,1)}), bf16[128,1024]{1,0:T(8,128)(2,1)}) %reduce-scatter.9.cloned.1.call-update) | async-done | bytes 262160 | tf_op jit(solution)/shard_map/reduce_scatter | solution.py:97
  156.1 17.6 %all_to_all.41 = bf16[4,64,2048]{2,1,0:T(8,128)(2,1)} all-to-all(bf16[4,64,2048]{2,1,0:T(8,128)(2,1)S(1)} %bitcast.155), channel_id=1, replica_groups=mesh['dp'=8,'expert'=4] {'expert'}, dimensions={0} | all-to-all | bytes 2097152 | tf_op jit(solution)/shard_map/all_to_all | solution.py:102
  174.0 8.4 all_to_all.42
  185.3 113.0 %all-gather.19.cloned.1.call-done = bf16[2048,2048]{1,0:T(8,128)(2,1)} async-done(((bf16[256,2048]{1,0:T(8,128)(2,1)}), bf16[2048,2048]{1,0:T(8,128)(2,1)}) %all-gather.19.cloned.1.call-update) | async-done | bytes 8388624 | tf_op jit(solution)/shard_map/all_gather | solution.py:105
  298.3 4.8 fusion.14
  303.1 5.0 fusion.7
  308.1 4.4 convolution_convert_fusion
  312.5 4.2 convolution_convert_fusion.1
  316.8 8.4 pad_maximum_fusion
  325.4 22.7 %all-gather.15.cloned.1.call-done = bf16[1024,1024]{1,0:T(8,128)(2,1)} async-done(((bf16[128,1024]{1,0:T(8,128)(2,1)}), bf16[1024,1024]{1,0:T(8,128)(2,1)}) %all-gather.15.cloned.1.call-update) | async-done | bytes 2097168 | tf_op jit(solution)/shard_map/all_gather | solution.py:105
  348.2 23.1 %all-gather.13.cloned.1.call-done = bf16[512,2048]{1,0:T(8,128)(2,1)} async-done(((bf16[128,2048]{1,0:T(8,128)(2,1)}), bf16[512,2048]{1,0:T(8,128)(2,1)}) %all-gather.13.cloned.1.call-update) | async-done | bytes 2097168 | tf_op jit(solution)/shard_map/all_gather | solution.py:94
  371.3 4.6 fusion.51
  375.9 46.6 %all-gather.17.cloned.1.call-done = bf16[1024,1024]{1,0:T(8,128)(2,1)} async-done(((bf16[128,1024]{1,0:T(8,128)(2,1)}), bf16[1024,1024]{1,0:T(8,128)(2,1)}) %all-gather.17.cloned.1.call-update) | async-done | bytes 2097168 | tf_op jit(solution)/shard_map/all_gather | solution.py:105
  422.5 4.7 fusion.25
  432.8 139.7 %reduce-scatter.13.cloned.1.call-done = bf16[256,2048]{0,1:T(8,128)(2,1)} async-done(((bf16[2048,2048]{0,1:T(8,128)(2,1)}), bf16[256,2048]{0,1:T(8,128)(2,1)}) %reduce-scatter.13.cloned.1.call-update) | async-done | bytes 1048592 | tf_op jit(solution)/shard_map/reduce_scatter | solution.py:108
  572.6 2.2 copy.104
  574.8 3.5 all-to-all-start.4
  578.4 27.6 %reduce-scatter.11.cloned.1.call-done = bf16[128,2048]{1,0:T(8,128)(2,1)} async-done(((bf16[512,2048]{1,0:T(8,128)(2,1)}), bf16[128,2048]{1,0:T(8,128)(2,1)}) %reduce-scatter.11.cloned.1.call-update) | async-done | bytes 524304 | tf_op jit(solution)/shard_map/reduce_scatter | solution.py:97
  612.2 3.8 convolution_convert_fusion.4
  616.1 4.4 convolution_convert_fusion.3
  620.6 8.4 all-gather.21.cloned.1.call-done
  631.6 3.5 all-to-all-start.6
  635.7 3.1 multiply_reduce_fusion
  645.2 3.2 convolution_convert_fusion.12
  650.5 51.2 %reduce-scatter.21.cloned.1.call-done = bf16[128,1024]{1,0:T(8,128)(2,1)} async-done(((bf16[1024,1024]{1,0:T(8,128)(2,1)}), bf16[128,1024]{1,0:T(8,128)(2,1)}) %reduce-scatter.21.cloned.1.call-update) | async-done | bytes 262160 | tf_op jit(solution)/shard_map/reduce_scatter | solution.py:108
  703.4 3.5 all-to-all-start.7
  707.2 65.3 %reduce-scatter.23.cloned.1.call-done = bf16[128,1024]{1,0:T(8,128)(2,1)} async-done(((bf16[1024,1024]{1,0:T(8,128)(2,1)}), bf16[128,1024]{1,0:T(8,128)(2,1)}) %reduce-scatter.23.cloned.1.call-update) | async-done | bytes 262160 | tf_op jit(solution)/shard_map/reduce_scatter | solution.py:108
  775.7 2.2 convolution_convert_fusion.5
  777.9 5.9 fusion.32
  783.9 3.5 copy.113
  787.4 4.5 fusion.29
  792.0 3.5 copy.112
  795.4 2.7 pad_maximum_fusion.10
  798.5 39.0 %reduce-scatter.19.cloned.1.call-done = bf16[32,1024]{1,0:T(8,128)(2,1)} async-done(((bf16[256,1024]{1,0:T(8,128)(2,1)}), bf16[32,1024]{1,0:T(8,128)(2,1)}) %reduce-scatter.19.cloned.1.call-update) | async-done | bytes 65552 | tf_op jit(solution)/shard_map/reduce_scatter | solution.py:108
  839.0 24.7 %reduce-scatter.15.cloned.1.call-done = bf16[128,1024]{1,0:T(8,128)(2,1)} async-done(((bf16[512,1024]{1,0:T(8,128)(2,1)}), bf16[128,1024]{1,0:T(8,128)(2,1)}) %reduce-scatter.15.cloned.1.call-update) | async-done | bytes 262160 | tf_op jit(solution)/shard_map/reduce_scatter | solution.py:97
  865.0 40.0 %all-reduce = (f32[8,1024]{1,0:T(8,128)S(1)}, f32[4]{0:T(128)S(1)}) all-reduce(f32[8,1024]{1,0:T(8,128)S(1)} %pad_maximum_fusion.8, f32[4]{0:T(128)S(1)} %pad_maximum_fusion.10), channel_id=1, replica_groups=mesh['dp'=8,'expert'=4] {'dp','expert'}, use_global_device_ids=true, to_apply=%region_26.27 | all-reduce | flops 8196 | bytes 65568 | tf_op jit(solution)/shard_map/psum | solution.py:303
  908.8 24.0 %reduce-scatter.17.cloned.1.call-done = bf16[128,768]{1,0:T(8,128)(2,1)} async-done(((bf16[1024,768]{1,0:T(8,128)(2,1)}), bf16[128,768]{1,0:T(8,128)(2,1)}) %reduce-scatter.17.cloned.1.call-update) | async-done | bytes 196624 | tf_op jit(solution)/shard_map/reduce_scatter | solution.py:108
  934.6 3.4 all-to-all-start.5
  938.5 4.7 all-to-all-done.5
  (202 shorter events, 57.3 us)
Async XLA Ops:
  7.2 291.1 %copy-start = (bf16[512,1,1024]{2,0,1:T(8,128)(2,1)S(1)}, bf16[512,1,1024]{2,0,1:T(8,128)(2,1)}, u32[]{:S(2)}) copy-start(bf16[512,1,1024]{2,0,1:T(8,128)(2,1)} %param.26) | copy-start | bytes 3145732
  7.2 60.7 %copy-start.26 = (bf16[32,1024]{1,0:T(8,128)(2,1)S(1)}, bf16[32,1024]{1,0:T(8,128)(2,1)}, u32[]{:S(2)}) copy-start(bf16[32,1024]{1,0:T(8,128)(2,1)} %param.20) | copy-start | bytes 196612
  7.2 106.8 %all-gather.9.cloned.1.call-start = ((), (), s32[]{:S(2)}) async-start(), calls=%async_computation.16 | async-start | bytes 1310720 | tf_op jit(solution)/shard_map/all_gather | solution.py:94
  55.8 60.6 %all-gather.11.cloned.1.call-start = ((), (), s32[]{:S(2)}) async-start(), calls=%async_computation.17 | async-start | bytes 1769472 | tf_op jit(solution)/shard_map/all_gather | solution.py:105
  101.7 12.3 %all-to-all-start.1 = ((bf16[4,64,1024]{2,1,0:T(8,128)(2,1)}), bf16[4,64,1024]{2,1,0:T(8,128)(2,1)S(1)}, u32[]{:S(2)}, u32[]{:S(2)}) async-start(bf16[4,64,1024]{2,1,0:T(8,128)(2,1)} %bitcast.11), calls=%async_computation.1 | async-start | bytes 1048576 | tf_op jit(solution)/shard_map/all_to_all | solution.py:102
  105.2 46.3 %reduce-scatter.9.cloned.1.call-start = ((), (), s32[]{:S(2)}) async-start(), calls=%async_computation.18 | async-start | bytes 1310720 | tf_op jit(solution)/shard_map/reduce_scatter | solution.py:97
  114.0 12.0 %copy-start.9 = (bf16[2,4,32,1024]{3,2,1,0:T(8,128)(2,1)}, bf16[2,4,32,1024]{3,2,1,0:T(8,128)(2,1)S(1)}, u32[]{:S(2)}) copy-start(bf16[2,4,32,1024]{3,2,1,0:T(8,128)(2,1)S(1)} %copy.102) | copy-start | bytes 1572868
  119.3 4.0 copy-start.16
  119.5 3.8 copy-start.18
  119.6 3.6 copy-start.24
  126.0 25.5 %copy-start.2 = (bf16[128,1024]{1,0:T(8,128)(2,1)S(1)}, bf16[128,1024]{1,0:T(8,128)(2,1)}, u32[]{:S(2)}) copy-start(bf16[128,1024]{1,0:T(8,128)(2,1)} %param.14) | copy-start | bytes 786436
  128.1 27.3 %copy-start.7 = (bf16[128,1024]{1,0:T(8,128)(2,1)S(1)}, bf16[128,1024]{1,0:T(8,128)(2,1)}, u32[]{:S(2)}) copy-start(bf16[128,1024]{1,0:T(8,128)(2,1)} %param.15) | copy-start | bytes 786436
  128.1 170.2 %all-gather.19.cloned.1.call-start = ((), (), s32[]{:S(2)}) async-start(), calls=%async_computation.23 | async-start | bytes 9437184 | tf_op jit(solution)/shard_map/all_gather | solution.py:105
  154.8 28.4 %copy-start.3 = (bf16[128,1024]{1,0:T(8,128)(2,1)}, bf16[128,1024]{1,0:T(8,128)(2,1)S(1)}, u32[]{:S(2)}) copy-start(bf16[128,1024]{1,0:T(8,128)(2,1)S(1)} %multiply_convert_fusion.3) | copy-start | bytes 786436
  155.5 18.2 %copy-start.23 = (bf16[32,4096]{1,0:T(8,128)(2,1)S(1)}, bf16[32,4096]{1,0:T(8,128)(2,1)}, u32[]{:S(2)}) copy-start(bf16[32,4096]{1,0:T(8,128)(2,1)} %param.22) | copy-start | bytes 786436
  173.7 174.5 %all-gather.15.cloned.1.call-start = ((), (), s32[]{:S(2)}) async-start(), calls=%async_computation.20 | async-start | bytes 2359296 | tf_op jit(solution)/shard_map/all_gather | solution.py:105
  183.1 188.1 %all-gather.13.cloned.1.call-start = ((), (), s32[]{:S(2)}) async-start(), calls=%async_computation.19 | async-start | bytes 2621440 | tf_op jit(solution)/shard_map/all_gather | solution.py:94
  184.1 238.5 %all-gather.17.cloned.1.call-start = ((), (), s32[]{:S(2)}) async-start(), calls=%async_computation.21 | async-start | bytes 2359296 | tf_op jit(solution)/shard_map/all_gather | solution.py:105
  184.8 118.3 %copy-start.34 = (bf16[512,1,1024]{2,0,1:T(8,128)(2,1)S(1)}, bf16[512,1,1024]{2,0,1:T(8,128)(2,1)}, u32[]{:S(2)}) copy-start(bf16[512,1,1024]{2,0,1:T(8,128)(2,1)} %param.27) | copy-start | bytes 3145732
  184.8 387.7 %reduce-scatter.13.cloned.1.call-start = ((), (), s32[]{:S(2)}) async-start(), calls=%async_computation.24 | async-start | bytes 9437184 | tf_op jit(solution)/shard_map/reduce_scatter | solution.py:108
  298.3 4.8 copy-start.28
  303.1 9.4 copy-start.38
  308.1 4.5 copy-start.40
  325.2 280.8 %reduce-scatter.11.cloned.1.call-start = ((), (), s32[]{:S(2)}) async-start(), calls=%async_computation.22 | async-start | bytes 2621440 | tf_op jit(solution)/shard_map/reduce_scatter | solution.py:97
  371.3 51.2 %copy-start.29 = (bf16[512,2048]{1,0:T(8,128)(2,1)S(1)}, bf16[512,2048]{1,0:T(8,128)(2,1)}, u32[]{:S(2)}) copy-start(bf16[512,2048]{1,0:T(8,128)(2,1)} %all-gather.13.cloned.1.call-done) | copy-start | bytes 6291460
  422.5 4.7 copy-start.31
  574.8 32.3 %all-to-all-start.4 = ((bf16[4,64,2048]{2,1,0:T(8,128)(2,1)}), bf16[4,64,2048]{2,1,0:T(8,128)(2,1)S(1)}, u32[]{:S(2)}, u32[]{:S(2)}) async-start(bf16[4,64,2048]{2,1,0:T(8,128)(2,1)} %bitcast.27), calls=%async_computation.7 | async-start | bytes 2097152 | tf_op jit(solution)/shard_map/all_to_all | solution.py:102
  578.3 29.1 %copy-start.5 = (bf16[128,1024]{1,0:T(8,128)(2,1)S(1)}, bf16[128,1024]{1,0:T(8,128)(2,1)}, u32[]{:S(2)}) copy-start(bf16[128,1024]{1,0:T(8,128)(2,1)} %reduce-scatter.9.cloned.1.call-done) | copy-start | bytes 786436
  578.3 29.1 %copy-start.8 = (bf16[128,1024]{1,0:T(8,128)(2,1)S(1)}, bf16[128,1024]{1,0:T(8,128)(2,1)}, u32[]{:S(2)}) copy-start(bf16[128,1024]{1,0:T(8,128)(2,1)} %param.15) | copy-start | bytes 786436
  578.3 50.7 %all-gather.21.cloned.1.call-start = ((), (), s32[]{:S(2)}) async-start(), calls=%async_computation.25 | async-start | bytes 1310720 | tf_op jit(solution)/shard_map/all_gather | solution.py:94
  612.1 89.5 %reduce-scatter.21.cloned.1.call-start = ((), (), s32[]{:S(2)}) async-start(), calls=%async_computation.29 | async-start | bytes 2359296 | tf_op jit(solution)/shard_map/reduce_scatter | solution.py:108
  616.1 156.4 %reduce-scatter.23.cloned.1.call-start = ((), (), s32[]{:S(2)}) async-start(), calls=%async_computation.30 | async-start | bytes 2359296 | tf_op jit(solution)/shard_map/reduce_scatter | solution.py:108
  620.6 8.5 copy-start.14
  620.6 14.6 %copy-start.10 = (bf16[2,4,32,1024]{3,2,1,0:T(8,128)(2,1)S(1)}, bf16[2,4,32,1024]{3,2,1,0:T(8,128)(2,1)}, u32[]{:S(2)}) copy-start(bf16[2,4,32,1024]{3,2,1,0:T(8,128)(2,1)} %copy-done.9) | copy-start | bytes 1572868
  629.0 6.1 copy-start.15
  630.8 4.9 copy-start.25
  631.6 12.3 %all-to-all-start.6 = ((bf16[4,2,32,1024]{3,2,1,0:T(8,128)(2,1)}), bf16[4,2,32,1024]{3,2,1,0:T(8,128)(2,1)S(1)}, u32[]{:S(2)}, u32[]{:S(2)}) async-start(bf16[4,2,32,1024]{3,2,1,0:T(8,128)(2,1)} %bitcast.149), calls=%async_computation.11 | async-start | bytes 1048576 | tf_op jit(solution)/shard_map/all_to_all | solution.py:102
  635.1 202.4 %reduce-scatter.19.cloned.1.call-start = ((), (), s32[]{:S(2)}) async-start(), calls=%async_computation.28 | async-start | bytes 589824 | tf_op jit(solution)/shard_map/reduce_scatter | solution.py:108
  640.4 4.3 copy-start.17
  644.7 219.1 %reduce-scatter.15.cloned.1.call-start = ((), (), s32[]{:S(2)}) async-start(), calls=%async_computation.26 | async-start | bytes 1310720 | tf_op jit(solution)/shard_map/reduce_scatter | solution.py:97
  703.4 72.3 %copy-start.22 = (bf16[4,64,512]{2,1,0:T(8,128)(2,1)S(1)}, bf16[4,64,512]{2,1,0:T(8,128)(2,1)}, u32[]{:S(2)}) copy-start(bf16[4,64,512]{2,1,0:T(8,128)(2,1)} %copy-done.21) | copy-start | bytes 786436
  703.4 72.3 %copy-start.35 = (bf16[512,1024]{1,0:T(8,128)(2,1)S(1)}, bf16[512,1024]{1,0:T(8,128)(2,1)}, u32[]{:S(2)}) copy-start(bf16[512,1024]{1,0:T(8,128)(2,1)} %all-gather.9.cloned.1.call-done) | copy-start | bytes 3145732
  703.4 70.9 %all-to-all-start.7 = ((bf16[4,32,8,128]{3,2,1,0:T(8,128)(2,1)}), bf16[4,32,8,128]{3,2,1,0:T(8,128)(2,1)S(1)}, u32[]{:S(2)}, u32[]{:S(2)}) async-start(bf16[4,32,8,128]{3,2,1,0:T(8,128)(2,1)} %bitcast.74), calls=%async_computation.14 | async-start | bytes 524288 | tf_op jit(solution)/shard_map/all_to_all | solution.py:102
  706.9 225.9 %reduce-scatter.17.cloned.1.call-start = ((), (), s32[]{:S(2)}) async-start(), calls=%async_computation.27 | async-start | bytes 1769472 | tf_op jit(solution)/shard_map/reduce_scatter | solution.py:108
  791.9 6.2 copy-start.4
  791.9 114.8 %copy-start.11 = (f32[128,1024]{1,0:T(8,128)S(1)}, f32[128,1024]{1,0:T(8,128)}, u32[]{:S(2)}) copy-start(f32[128,1024]{1,0:T(8,128)} %get-tuple-element.112) | copy-start | bytes 1572868
  906.7 37.7 %copy-start.1 = (bf16[512,1,1024]{2,0,1:T(8,128)(2,1)S(1)}, bf16[512,1,1024]{2,0,1:T(8,128)(2,1)}, u32[]{:S(2)}) copy-start(bf16[512,1,1024]{2,0,1:T(8,128)(2,1)} %param.26) | copy-start | bytes 3145732
  934.6 8.6 all-to-all-start.5
  (14 other events, 33.1 us)
Sparse Core Ops, SparseCore 0:
  55.9 14.9 all-gather.8
  73.6 42.6 all-gather.10
  128.2 23.1 reduce-scatter.8
  173.8 124.4 all-gather.18
  300.9 47.2 all-gather.14
  350.1 21.0 all-gather.12
  373.4 49.0 all-gather.16
  426.1 146.3 reduce-scatter.12
  575.7 30.2 reduce-scatter.10
  612.3 16.6 all-gather.20
  633.1 68.4 reduce-scatter.20
  705.0 67.3 reduce-scatter.22
  775.8 61.6 reduce-scatter.18
  839.9 23.7 reduce-scatter.14
  867.0 65.7 reduce-scatter.16
where the time goes:
time: 958 us; the launch traced here: 951 us
  waiting for transfers between devices  626 us (65%)
  blocking collectives  153 us (16%)
  matrix products  78 us (8%)
  other arithmetic  34 us (4%)
  local copies, waits for them, and re-layouts  25.2 us (3%)
  starting transfers between devices  18.8 us (2%)
  between operations  15.8 us (2%)
    reduce_scatter x5, waiting for transfers between devices, scatter_dp(): lax.psum_scatter(rows.astype(jnp.bfloat16), 'dp', scatter_dimension=0, ti...  319 us
    all_gather x4, waiting for transfers between devices, gather_dp(): return lax.all_gather(rows, 'dp', axis=0, tiled=True)  185 us
    reduce_scatter x3, waiting for transfers between devices, fold(): lax.psum_scatter(partial_sums.astype(jnp.bfloat16), 'expert', scatter_dim...  75.4 us
    all_gather x1, blocking collectives, per_device(): lax.all_gather(jnp.concatenate([norm1_gain[:, None], norm2_gain[:, None],...  43.4 us
    psum x1, blocking collectives, per_device(): lax.psum((jnp.concatenate([grad_gain_one[None], grad_gain_two[None], grad...  40 us
    all_to_all x3, blocking collectives, swap(): lax.all_to_all(blocks, 'expert', split_axis=0, concat_axis=0, tiled=True)  36.1 us
    all_gather x1, blocking collectives, gather_dp(): return lax.all_gather(rows, 'dp', axis=0, tiled=True)  33.8 us
    all_gather x3, waiting for transfers between devices, spread(): return lax.all_gather(rows_low, 'expert', axis=0, tiled=True)  31.6 us
  transfers between devices with their start and end apart: 20, of which 17 were waited for; matrix products, arithmetic and copies ran while one was open for 11% of the time, Pallas kernels for 0%

commit v1 on v0

--- a/solution.py
+++ b/solution.py
@@ -9,6 +9,19 @@
 HIGHEST = lax.Precision.HIGHEST
 ROWS_AXIS = (((0,), (0,)), ((), ()))
 COLS_AXIS = (((1,), (1,)), ((), ()))
+
+
+def ring_gather(x, axis, dim):
+    ways = lax.axis_size(axis)
+    up = [(d, (d + 1) % ways) for d in range(ways)]
+    down = [(d, (d - 1) % ways) for d in range(ways)]
+    earlier, later = ([x], [x])
+    for _ in range(ways // 2):
+        earlier.append(lax.ppermute(earlier[-1], axis, up))
+    for _ in range((ways - 1) // 2):
+        later.append(lax.ppermute(later[-1], axis, down))
+    line = jnp.concatenate([*earlier[::-1], *later[1:]], axis=dim)
+    return jnp.roll(line, (lax.axis_index(axis) - ways // 2) * x.shape[dim], axis=dim)
 
 
 def layer_norm(values, norm_gain):
@@ -91,7 +104,7 @@
     ff_own = replicas * ff_share
 
     def spread(rows_low):
-        return lax.all_gather(rows_low, "expert", axis=0, tiled=True)
+        return ring_gather(rows_low, "expert", 0)
 
     def fold(partial_sums):
         return lax.psum_scatter(

time: 958 us -> 915 us (0.955)
  waiting for transfers between devices: 626 us -> 559 us
    ppermute x0 -> x9, waiting for transfers between devices: none -> 34.5 us  [the longest x6 31.6 us: ring_gather(): earlier.append(lax.ppermute(earlier[-1], axis, up))]
    all_gather x3 -> x0, waiting for transfers between devices: 31.6 us -> none  [spread(): return lax.all_gather(rows_low, 'expert', axis=0, tiled=True)]
    reduce_scatter x5, waiting for transfers between devices: 319 us -> 289 us  [scatter_dp(): lax.psum_scatter(rows.astype(jnp.bfloat16), 'dp', scatter_dimension=0, ti...]
    all_gather x4, waiting for transfers between devices: 185 us -> 155 us  [gather_dp(): return lax.all_gather(rows, 'dp', axis=0, tiled=True)]
  transfers between devices with their start and end apart: 20 -> 26, of which waited for: 17 -> 19; matrix products, arithmetic and copies ran while one was open for 11% -> 14% of each run, Pallas kernels for 0% -> 0%
where the time goes in v1:
time: 915 us; the launch traced here: 905 us
  waiting for transfers between devices  559 us (61%)
  blocking collectives  150 us (16%)
  matrix products  81.6 us (9%)
  other arithmetic  38.8 us (4%)
  local copies, waits for them, and re-layouts  34.4 us (4%)
  starting transfers between devices  25.2 us (3%)
  between operations  15.9 us (2%)
    reduce_scatter x5, waiting for transfers between devices, scatter_dp(): lax.psum_scatter(rows.astype(jnp.bfloat16), 'dp', scatter_dimension=0, ti...  289 us
    all_gather x4, waiting for transfers between devices, gather_dp(): return lax.all_gather(rows, 'dp', axis=0, tiled=True)  155 us
    reduce_scatter x3, waiting for transfers between devices, fold(): lax.psum_scatter(partial_sums.astype(jnp.bfloat16), 'expert', scatter_dim...  68.4 us
    all_gather x1, blocking collectives, per_device(): lax.all_gather(jnp.concatenate([norm1_gain[:, None], norm2_gain[:, None],...  41.4 us
    psum x1, blocking collectives, per_device(): lax.psum((jnp.concatenate([grad_gain_one[None], grad_gain_two[None], grad...  40 us
    all_to_all x3, blocking collectives, swap(): lax.all_to_all(blocks, 'expert', split_axis=0, concat_axis=0, tiled=True)  35.4 us
    all_gather x1, blocking collectives, gather_dp(): return lax.all_gather(rows, 'dp', axis=0, tiled=True)  33.2 us
    ppermute x6, waiting for transfers between devices, ring_gather(): earlier.append(lax.ppermute(earlier[-1], axis, up))  31.6 us
  transfers between devices with their start and end apart: 26, of which 19 were waited for; matrix products, arithmetic and copies ran while one was open for 14% of the time, Pallas kernels for 0%

profile of v1, /device:TPU:0, one launch (start us, length us, event | category | flops | bytes accessed | tf_op | source)
XLA Modules:
  0.0 905.3 jit_solution(13346867357379011866)
XLA Ops:
  8.5 9.4 %all_to_all.40 = bf16[4,32,3,256]{3,1,2,0:T(8,128)(2,1)S(1)} all-to-all(bf16[4,32,3,256]{3,1,2,0:T(8,128)(2,1)S(1)} %copy.96), channel_id=1, replica_groups=mesh['dp'=8,'expert'=4] {'expert'}, dimensions={0} | all-to-all | bytes 393216 | tf_op jit(solution)/shard_map/all_to_all | solution.py:115
  18.8 41.4 %all-gather = bf16[32,32,8]{1,2,0:T(8,128)(2,1)S(1)} all-gather(bf16[1,32,8]{1,2,0:T(8,128)(2,1)S(1)} %maximum_bitcast_fusion), channel_id=1, replica_groups=mesh['dp'=8,'expert'=4] {'dp','expert'}, dimensions={0}, use_global_device_ids=true | all-gather | bytes 16896 | tf_op jit(solution)/shard_map/all_gather | solution.py:123
  61.4 33.2 %all_gather.20 = bf16[256,1024]{1,0:T(8,128)(2,1)} all-gather(bf16[32,1024]{1,0:T(8,128)(2,1)S(1)} %copy-done.22), channel_id=1, replica_groups=mesh['dp'=8,'expert'=4] {'dp'}, dimensions={0}, use_global_device_ids=true | all-gather | bytes 589824 | tf_op jit(solution)/shard_map/all_gather | solution.py:118
  94.6 3.5 all-to-all-start.1
  101.4 6.0 all-to-all-done.1
  107.5 2.9 collective-permute-done.2
  112.0 4.3 fusion.48
  116.3 2.7 convolution_convert_fusion.10
  122.4 4.7 fusion.128
  131.5 21.7 %reduce-scatter.9.cloned.1.call-done = bf16[128,1024]{1,0:T(8,128)(2,1)} async-done(((bf16[512,1024]{1,0:T(8,128)(2,1)}), bf16[128,1024]{1,0:T(8,128)(2,1)}) %reduce-scatter.9.cloned.1.call-update) | async-done | bytes 262160 | tf_op jit(solution)/shard_map/reduce_scatter | solution.py:110
  157.9 17.6 %all_to_all.41 = bf16[4,64,2048]{2,1,0:T(8,128)(2,1)} all-to-all(bf16[4,64,2048]{2,1,0:T(8,128)(2,1)S(1)} %bitcast.154), channel_id=1, replica_groups=mesh['dp'=8,'expert'=4] {'expert'}, dimensions={0} | all-to-all | bytes 2097152 | tf_op jit(solution)/shard_map/all_to_all | solution.py:115
  175.8 8.4 all_to_all.42
  185.7 114.4 %all-gather.12.cloned.1.call-done = bf16[2048,2048]{1,0:T(8,128)(2,1)} async-done(((bf16[256,2048]{1,0:T(8,128)(2,1)}), bf16[2048,2048]{1,0:T(8,128)(2,1)}) %all-gather.12.cloned.1.call-update) | async-done | bytes 8388624 | tf_op jit(solution)/shard_map/all_gather | solution.py:118
  300.1 4.8 fusion.14
  305.0 4.9 fusion.7
  309.9 4.4 convolution_convert_fusion
  314.4 4.2 convolution_convert_fusion.1
  318.6 8.4 pad_maximum_fusion
  327.2 8.6 collective-permute-done.3
  337.7 10.1 %collective-permute-done.4 = bf16[128,2048]{1,0:T(8,128)(2,1)S(1)} collective-permute-done((bf16[128,2048]{1,0:T(8,128)(2,1)S(1)}, bf16[128,2048]{1,0:T(8,128)(2,1)S(1)}, u32[]{:S(2)}, u32[]{:S(2)}) %collective-permute-start.4) | collective-permute-done | bytes 524320 | tf_op jit(solution)/shard_map/ppermute | solution.py:20
  354.6 4.5 fusion.60
  359.1 40.5 %all-gather.10.cloned.1.call-done = bf16[1024,1024]{1,0:T(8,128)(2,1)} async-done(((bf16[128,1024]{1,0:T(8,128)(2,1)}), bf16[1024,1024]{1,0:T(8,128)(2,1)}) %all-gather.10.cloned.1.call-update) | async-done | bytes 2097168 | tf_op jit(solution)/shard_map/all_gather | solution.py:118
  399.6 5.0 fusion.25
  409.9 3.8 convolution_convert_fusion.4
  413.8 135.7 %reduce-scatter.13.cloned.1.call-done = bf16[256,2048]{0,1:T(8,128)(2,1)} async-done(((bf16[2048,2048]{0,1:T(8,128)(2,1)}), bf16[256,2048]{0,1:T(8,128)(2,1)}) %reduce-scatter.13.cloned.1.call-update) | async-done | bytes 1048592 | tf_op jit(solution)/shard_map/reduce_scatter | solution.py:121
  551.7 4.3 all-to-all-start.4
  556.1 5.0 convolution_convert_fusion.3
  561.1 21.8 %reduce-scatter.11.cloned.1.call-done = bf16[128,2048]{1,0:T(8,128)(2,1)} async-done(((bf16[512,2048]{1,0:T(8,128)(2,1)}), bf16[128,2048]{1,0:T(8,128)(2,1)}) %reduce-scatter.11.cloned.1.call-update) | async-done | bytes 524304 | tf_op jit(solution)/shard_map/reduce_scatter | solution.py:110
  591.2 6.2 collective-permute-done.6
  597.8 5.8 collective-permute-done.7
  603.6 4.2 fusion.41
  609.1 3.5 all-to-all-start.6
  613.1 3.1 multiply_reduce_fusion
  624.3 3.1 convolution_convert_fusion.12
  629.5 25.2 %reduce-scatter.21.cloned.1.call-done = bf16[128,1024]{1,0:T(8,128)(2,1)} async-done(((bf16[1024,1024]{1,0:T(8,128)(2,1)}), bf16[128,1024]{1,0:T(8,128)(2,1)}) %reduce-scatter.21.cloned.1.call-update) | async-done | bytes 262160 | tf_op jit(solution)/shard_map/reduce_scatter | solution.py:121
  656.4 3.5 all-to-all-start.7
  660.2 65.5 %reduce-scatter.23.cloned.1.call-done = bf16[128,1024]{1,0:T(8,128)(2,1)} async-done(((bf16[1024,1024]{1,0:T(8,128)(2,1)}), bf16[128,1024]{1,0:T(8,128)(2,1)}) %reduce-scatter.23.cloned.1.call-update) | async-done | bytes 262160 | tf_op jit(solution)/shard_map/reduce_scatter | solution.py:121
  728.9 3.3 convolution_convert_fusion.5
  732.2 5.9 fusion.32
  738.2 3.5 copy.113
  741.7 4.5 fusion.29
  746.2 3.5 copy.112
  752.8 38.5 %reduce-scatter.19.cloned.1.call-done = bf16[32,1024]{1,0:T(8,128)(2,1)} async-done(((bf16[256,1024]{1,0:T(8,128)(2,1)}), bf16[32,1024]{1,0:T(8,128)(2,1)}) %reduce-scatter.19.cloned.1.call-update) | async-done | bytes 65552 | tf_op jit(solution)/shard_map/reduce_scatter | solution.py:121
  792.8 24.9 %reduce-scatter.15.cloned.1.call-done = bf16[128,1024]{1,0:T(8,128)(2,1)} async-done(((bf16[512,1024]{1,0:T(8,128)(2,1)}), bf16[128,1024]{1,0:T(8,128)(2,1)}) %reduce-scatter.15.cloned.1.call-update) | async-done | bytes 262160 | tf_op jit(solution)/shard_map/reduce_scatter | solution.py:110
  818.9 40.0 %all-reduce = (f32[8,1024]{1,0:T(8,128)S(1)}, f32[4]{0:T(128)S(1)}) all-reduce(f32[8,1024]{1,0:T(8,128)S(1)} %pad_maximum_fusion.8, f32[4]{0:T(128)S(1)} %pad_maximum_fusion.10), channel_id=1, replica_groups=mesh['dp'=8,'expert'=4] {'dp','expert'}, use_global_device_ids=true, to_apply=%region_26.28 | all-reduce | flops 8196 | bytes 65568 | tf_op jit(solution)/shard_map/psum | solution.py:316
  862.7 23.9 %reduce-scatter.17.cloned.1.call-done = bf16[128,768]{1,0:T(8,128)(2,1)} async-done(((bf16[1024,768]{1,0:T(8,128)(2,1)}), bf16[128,768]{1,0:T(8,128)(2,1)}) %reduce-scatter.17.cloned.1.call-update) | async-done | bytes 196624 | tf_op jit(solution)/shard_map/reduce_scatter | solution.py:121
  888.4 3.4 all-to-all-start.5
  892.4 4.7 all-to-all-done.5
  (217 shorter events, 76.9 us)
Async XLA Ops:
  7.2 292.9 %copy-start = (bf16[512,1,1024]{2,0,1:T(8,128)(2,1)S(1)}, bf16[512,1,1024]{2,0,1:T(8,128)(2,1)}, u32[]{:S(2)}) copy-start(bf16[512,1,1024]{2,0,1:T(8,128)(2,1)} %param.28) | copy-start | bytes 3145732
  7.2 11.6 %copy-start.25 = (bf16[32,2]{0,1:T(2,128)(2,1)S(1)}, bf16[32,2]{0,1:T(2,128)(2,1)}, u32[]{:S(2)}) copy-start(bf16[32,2]{0,1:T(2,128)(2,1)} %param.27) | copy-start | bytes 388
  7.2 11.6 %copy-start.24 = (bf16[32,4]{0,1:T(4,128)(2,1)S(1)}, bf16[32,4]{0,1:T(4,128)(2,1)}, u32[]{:S(2)}) copy-start(bf16[32,4]{0,1:T(4,128)(2,1)} %param.26) | copy-start | bytes 772
  7.2 11.6 %copy-start.26 = (bf16[32]{0:T(256)(128)(2,1)S(1)}, bf16[32]{0:T(256)(128)(2,1)}, u32[]{:S(2)}) copy-start(bf16[32]{0:T(256)(128)(2,1)} %param.23) | copy-start | bytes 196
  7.2 11.6 %copy-start.27 = (bf16[32]{0:T(256)(128)(2,1)S(1)}, bf16[32]{0:T(256)(128)(2,1)}, u32[]{:S(2)}) copy-start(bf16[32]{0:T(256)(128)(2,1)} %param.20) | copy-start | bytes 196
  7.2 53.1 %copy-start.2 = (bf16[128,1024]{1,0:T(8,128)(2,1)S(1)}, bf16[128,1024]{1,0:T(8,128)(2,1)}, u32[]{:S(2)}) copy-start(bf16[128,1024]{1,0:T(8,128)(2,1)} %param.16) | copy-start | bytes 786436
  7.2 54.1 %copy-start.22 = (bf16[32,1024]{1,0:T(8,128)(2,1)S(1)}, bf16[32,1024]{1,0:T(8,128)(2,1)}, u32[]{:S(2)}) copy-start(bf16[32,1024]{1,0:T(8,128)(2,1)} %param.22) | copy-start | bytes 196612
  7.3 109.0 %all-gather.6.cloned.1.call-start = ((), (), s32[]{:S(2)}) async-start(), calls=%async_computation.16 | async-start | bytes 1769472 | tf_op jit(solution)/shard_map/all_gather | solution.py:118
  61.0 39.5 %collective-permute-start = (bf16[128,1024]{1,0:T(8,128)(2,1)S(1)}, bf16[128,1024]{1,0:T(8,128)(2,1)S(1)}, u32[]{:S(2)}, u32[]{:S(2)}) collective-permute-start(bf16[128,1024]{1,0:T(8,128)(2,1)S(1)} %fusion.74), channel_id=1, source_target_pairs={{0,1},{1,2},{2,3},{3,0},{4,5},{5,6},{6,7},{7,4},{8,9},{9,10},{10,1... | collective-permute-start | bytes 786440 | tf_op jit(solution)/shard_map/ppermute | solution.py:20
  94.6 12.8 %all-to-all-start.1 = ((bf16[4,64,1024]{2,1,0:T(8,128)(2,1)}), bf16[4,64,1024]{2,1,0:T(8,128)(2,1)S(1)}, u32[]{:S(2)}, u32[]{:S(2)}) async-start(bf16[4,64,1024]{2,1,0:T(8,128)(2,1)} %bitcast.11), calls=%async_computation.1 | async-start | bytes 1048576 | tf_op jit(solution)/shard_map/all_to_all | solution.py:115
  98.1 55.2 %reduce-scatter.9.cloned.1.call-start = ((), (), s32[]{:S(2)}) async-start(), calls=%async_computation.17 | async-start | bytes 1310720 | tf_op jit(solution)/shard_map/reduce_scatter | solution.py:110
  98.1 12.3 %collective-permute-start.2 = (bf16[128,1024]{1,0:T(8,128)(2,1)S(1)}, bf16[128,1024]{1,0:T(8,128)(2,1)S(1)}, u32[]{:S(2)}, u32[]{:S(2)}) collective-permute-start(bf16[128,1024]{1,0:T(8,128)(2,1)S(1)} %fusion.74), channel_id=1, source_target_pairs={{0,3},{1,0},{2,1},{3,2},{4,7},{5,4},{6,5},{7,6},{8,11},{9,8},{10,9... | collective-permute-start | bytes 786440 | tf_op jit(solution)/shard_map/ppermute | solution.py:22
  100.5 11.6 %collective-permute-start.1 = (bf16[128,1024]{1,0:T(8,128)(2,1)S(1)}, bf16[128,1024]{1,0:T(8,128)(2,1)}, u32[]{:S(2)}, u32[]{:S(2)}) collective-permute-start(bf16[128,1024]{1,0:T(8,128)(2,1)S(1)} %collective-permute-done), channel_id=1, source_target_pairs={{0,1},{1,2},{2,3},{3,0},{4,5},{5,6},{6,7},{7,4},{8,9},{9,10},{10,1... | collective-permute-start | bytes 786440 | tf_op jit(solution)/shard_map/ppermute | solution.py:20
  121.0 6.1 copy-start.12
  122.2 4.9 copy-start.14
  129.8 25.7 %copy-start.8 = (bf16[4,64,512]{2,1,0:T(8,128)(2,1)}, bf16[4,64,512]{2,1,0:T(8,128)(2,1)S(1)}, u32[]{:S(2)}) copy-start(bf16[4,64,512]{2,1,0:T(8,128)(2,1)S(1)} %convolution_convert_fusion.14) | copy-start | bytes 786436
  131.2 25.9 %copy-start.6 = (bf16[128,1024]{1,0:T(8,128)(2,1)S(1)}, bf16[128,1024]{1,0:T(8,128)(2,1)}, u32[]{:S(2)}) copy-start(bf16[128,1024]{1,0:T(8,128)(2,1)} %param.17) | copy-start | bytes 786436
  131.3 168.8 %all-gather.12.cloned.1.call-start = ((), (), s32[]{:S(2)}) async-start(), calls=%async_computation.21 | async-start | bytes 9437184 | tf_op jit(solution)/shard_map/all_gather | solution.py:118
  157.3 18.2 %copy-start.19 = (bf16[32,4096]{1,0:T(8,128)(2,1)S(1)}, bf16[32,4096]{1,0:T(8,128)(2,1)}, u32[]{:S(2)}) copy-start(bf16[32,4096]{1,0:T(8,128)(2,1)} %param.24) | copy-start | bytes 786436
  175.5 179.1 %all-gather.8.cloned.1.call-start = ((), (), s32[]{:S(2)}) async-start(), calls=%async_computation.18 | async-start | bytes 2359296 | tf_op jit(solution)/shard_map/all_gather | solution.py:118
  184.9 214.7 %all-gather.10.cloned.1.call-start = ((), (), s32[]{:S(2)}) async-start(), calls=%async_computation.19 | async-start | bytes 2359296 | tf_op jit(solution)/shard_map/all_gather | solution.py:118
  185.5 364.0 %reduce-scatter.13.cloned.1.call-start = ((), (), s32[]{:S(2)}) async-start(), calls=%async_computation.22 | async-start | bytes 9437184 | tf_op jit(solution)/shard_map/reduce_scatter | solution.py:121
  300.1 4.8 copy-start.28
  300.1 4.9 copy-start.32
  305.0 9.4 %copy-start.37 = (f32[2048,512]{1,0:T(8,128)}, f32[2048,512]{1,0:T(8,128)S(1)}, u32[]{:S(2)}) copy-start(f32[2048,512]{1,0:T(8,128)S(1)} %fusion.14) | copy-start | bytes 12582916
  327.0 255.9 %reduce-scatter.11.cloned.1.call-start = ((), (), s32[]{:S(2)}) async-start(), calls=%async_computation.20 | async-start | bytes 2621440 | tf_op jit(solution)/shard_map/reduce_scatter | solution.py:110
  327.1 8.7 copy-start.16
  327.1 8.7 collective-permute-start.3
  335.8 12.0 %collective-permute-start.4 = (bf16[128,2048]{1,0:T(8,128)(2,1)S(1)}, bf16[128,2048]{1,0:T(8,128)(2,1)S(1)}, u32[]{:S(2)}, u32[]{:S(2)}) collective-permute-start(bf16[128,2048]{1,0:T(8,128)(2,1)S(1)} %collective-permute-done.3), channel_id=1, source_target_pairs={{0,1},{1,2},{2,3},{3,0},{4,5},{5,6},{6,7},{7,4},{8,9},{9,10},{10,1... | collective-permute-start | bytes 1572872 | tf_op jit(solution)/shard_map/ppermute | solution.py:20
  335.8 14.6 %collective-permute-start.5 = (bf16[128,2048]{1,0:T(8,128)(2,1)}, bf16[128,2048]{1,0:T(8,128)(2,1)S(1)}, u32[]{:S(2)}, u32[]{:S(2)}) collective-permute-start(bf16[128,2048]{1,0:T(8,128)(2,1)} %copy-done.16), channel_id=1, source_target_pairs={{0,3},{1,0},{2,1},{3,2},{4,7},{5,4},{6,5},{7,6},{8,11},{9,8},{10,9... | collective-permute-start | bytes 1572872 | tf_op jit(solution)/shard_map/ppermute | solution.py:22
  399.6 5.0 copy-start.29
  409.8 244.9 %reduce-scatter.21.cloned.1.call-start = ((), (), s32[]{:S(2)}) async-start(), calls=%async_computation.26 | async-start | bytes 2359296 | tf_op jit(solution)/shard_map/reduce_scatter | solution.py:121
  551.7 32.3 %all-to-all-start.4 = ((bf16[4,64,2048]{2,1,0:T(8,128)(2,1)}), bf16[4,64,2048]{2,1,0:T(8,128)(2,1)}, u32[]{:S(2)}, u32[]{:S(2)}) async-start(bf16[4,64,2048]{2,1,0:T(8,128)(2,1)} %bitcast.27), calls=%async_computation.7 | async-start | bytes 2097152 | tf_op jit(solution)/shard_map/all_to_all | solution.py:115
  556.0 169.7 %reduce-scatter.23.cloned.1.call-start = ((), (), s32[]{:S(2)}) async-start(), calls=%async_computation.27 | async-start | bytes 2359296 | tf_op jit(solution)/shard_map/reduce_scatter | solution.py:121
  561.1 24.6 %copy-start.4 = (bf16[128,1024]{1,0:T(8,128)(2,1)S(1)}, bf16[128,1024]{1,0:T(8,128)(2,1)}, u32[]{:S(2)}) copy-start(bf16[128,1024]{1,0:T(8,128)(2,1)} %reduce-scatter.9.cloned.1.call-done) | copy-start | bytes 786436
  589.1 18.6 %copy-start.9 = (bf16[4,64,512]{2,1,0:T(8,128)(2,1)S(1)}, bf16[4,64,512]{2,1,0:T(8,128)(2,1)}, u32[]{:S(2)}) copy-start(bf16[4,64,512]{2,1,0:T(8,128)(2,1)} %copy-done.8) | copy-start | bytes 786436
  589.4 8.0 collective-permute-start.6
  589.5 8.4 collective-permute-start.8
  597.4 6.2 collective-permute-start.7
  608.2 4.9 copy-start.21
  609.1 12.3 %all-to-all-start.6 = ((bf16[4,2,32,1024]{3,2,1,0:T(8,128)(2,1)}), bf16[4,2,32,1024]{3,2,1,0:T(8,128)(2,1)S(1)}, u32[]{:S(2)}, u32[]{:S(2)}) async-start(bf16[4,2,32,1024]{3,2,1,0:T(8,128)(2,1)} %bitcast.160), calls=%async_computation.11 | async-start | bytes 1048576 | tf_op jit(solution)/shard_map/all_to_all | solution.py:115
  612.6 178.7 %reduce-scatter.19.cloned.1.call-start = ((), (), s32[]{:S(2)}) async-start(), calls=%async_computation.25 | async-start | bytes 589824 | tf_op jit(solution)/shard_map/reduce_scatter | solution.py:121
  622.2 195.5 %reduce-scatter.15.cloned.1.call-start = ((), (), s32[]{:S(2)}) async-start(), calls=%async_computation.23 | async-start | bytes 1310720 | tf_op jit(solution)/shard_map/reduce_scatter | solution.py:110
  656.4 72.5 %copy-start.11 = (bf16[512,1024]{1,0:T(8,128)(2,1)S(1)}, bf16[512,1024]{1,0:T(8,128)(2,1)}, u32[]{:S(2)}) copy-start(bf16[512,1024]{1,0:T(8,128)(2,1)} %copy-done.10) | copy-start | bytes 3145732
  656.4 71.1 %all-to-all-start.7 = ((bf16[4,32,8,128]{3,2,1,0:T(8,128)(2,1)}), bf16[4,32,8,128]{3,2,1,0:T(8,128)(2,1)S(1)}, u32[]{:S(2)}, u32[]{:S(2)}) async-start(bf16[4,32,8,128]{3,2,1,0:T(8,128)(2,1)} %bitcast.74), calls=%async_computation.14 | async-start | bytes 524288 | tf_op jit(solution)/shard_map/all_to_all | solution.py:115
  660.0 226.7 %reduce-scatter.17.cloned.1.call-start = ((), (), s32[]{:S(2)}) async-start(), calls=%async_computation.24 | async-start | bytes 1769472 | tf_op jit(solution)/shard_map/reduce_scatter | solution.py:121
  860.6 37.7 %copy-start.1 = (bf16[512,1,1024]{2,0,1:T(8,128)(2,1)S(1)}, bf16[512,1,1024]{2,0,1:T(8,128)(2,1)}, u32[]{:S(2)}) copy-start(bf16[512,1,1024]{2,0,1:T(8,128)(2,1)} %param.28) | copy-start | bytes 3145732
  888.4 8.6 all-to-all-start.5
  (18 other events, 48.5 us)
Sparse Core Ops, SparseCore 0:
  18.9 44.5 all-gather.5
  131.4 21.8 reduce-scatter.8
  175.6 124.4 all-gather.11
  302.7 47.2 all-gather.7
  351.9 47.6 all-gather.9
  403.1 146.3 reduce-scatter.12
  552.6 30.2 reduce-scatter.10
  586.4 68.2 reduce-scatter.20
  658.3 67.4 reduce-scatter.22
  729.5 61.7 reduce-scatter.18
  793.8 23.7 reduce-scatter.14
  820.9 65.7 reduce-scatter.16
